TPU v7x, 32 devices: a whole 2x2x4 slice. The times are simulated.
32 devices in a mesh: dp: 4 (over y, x), seq: 8 (over z, core).
Axes of the slice: x: 2, y: 2, z: 4, core: 2. Of those that a mesh axis runs over, the one named last changes fastest.
Arguments:
- queries: bfloat16 [4, 1024, 2048], P('dp', 'seq'), may hold values from -6 to 6
- key_vectors: bfloat16 [4, 1024, 2048], P('dp', 'seq'), may hold values from -6 to 6
- values: bfloat16 [4, 1024, 2048], P('dp', 'seq'), may hold values from -6 to 6
- out_grad: bfloat16 [4, 1024, 2048], P('dp', 'seq'), may hold values from -6 to 6
- inputs: bfloat16 [4, 1024, 2048], P('dp', 'seq'), may hold values from -6 to 6
Outputs:
- query_grad: bfloat16 [4, 1024, 2048], P('dp', 'seq')
- key_grad: bfloat16 [4, 1024, 2048], P('dp', 'seq')
- value_grad: bfloat16 [4, 1024, 2048], P('dp', 'seq')
- weight_grad: float32 [2048, 2048], P('dp', 'seq')
All inputs are finite; a program needn't handle non-finite values.
Results may differ from a plain program's by a relative error of at most 0.025.
Values may be sent and summed in bfloat16 or wider, within the bound.
No kernel may reach another device: no remote copies, remote signals or barrier semaphores. Data moves between devices by JAX's collectives and lax.ppermute only.
A program may use at most 128 MiB of HBM per device.

v0:
```python
import jax
import jax.numpy as jnp
from jax import lax
from jax.sharding import PartitionSpec as P

HD = 128


def partner(value, axis, apart):
    return lax.ppermute(value, axis, [(i, i ^ 1 << apart) for i in range(lax.axis_size(axis))])


def body(queries, key_vectors, values, out_grad, inputs):
    seq_count = lax.axis_size("seq")
    groups = seq_count // 2
    parity = lax.axis_index("seq") % 2
    is_even = parity == 0
    tok_rows = queries.shape[1]
    half_rows = tok_rows // 2
    width = queries.shape[2]
    group_width = 2 * width // seq_count
    heads_here = group_width // HD
    model_width = inputs.shape[2]
    own_rows = seq_count * half_rows
    length = 2 * own_rows
    doc_rows = own_rows // 4
    block_rows = min(doc_rows, max(256, length // 16))
    block_count = own_rows // block_rows
    scale = HD ** (-0.5)

    def to_heads(array):
        return (
            array[0]
            .reshape(half_rows, 2, groups, group_width)
            .transpose(0, 2, 1, 3)
            .reshape(half_rows, seq_count, group_width)
        )

    moved = (
        lax.all_to_all(to_heads(queries), "seq", split_axis=1, concat_axis=0, tiled=True),
        lax.all_to_all(to_heads(key_vectors), "seq", split_axis=1, concat_axis=0, tiled=True),
        lax.all_to_all(to_heads(values), "seq", split_axis=1, concat_axis=0, tiled=True),
        lax.all_to_all(to_heads(out_grad), "seq", split_axis=1, concat_axis=0, tiled=True),
    )
    q_rows = moved[0].reshape(own_rows, group_width)
    k_rows = moved[1].reshape(own_rows, group_width)
    v_rows = moved[2].reshape(own_rows, group_width)
    g_rows = moved[3].reshape(own_rows, group_width)
    k_other, v_other = partner((k_rows, v_rows), "seq", 0)

    def in_order(mine, theirs):
        even_rows = jnp.where(is_even, mine, theirs)
        odd_rows = jnp.where(is_even, theirs, mine)
        return jnp.stack([even_rows, odd_rows], axis=1).reshape(2 * mine.shape[0], mine.shape[1])

    key_all = in_order(k_rows, k_other).reshape(length, heads_here, HD)
    value_all = in_order(v_rows, v_other).reshape(length, heads_here, HD)
    query_heads = q_rows.reshape(own_rows, heads_here, HD)
    grad_heads = g_rows.reshape(own_rows, heads_here, HD)
    key_total = jnp.zeros((length, heads_here, HD), jnp.float32)
    value_total = jnp.zeros((length, heads_here, HD), jnp.float32)
    query_parts = []
    for block in range(block_count):
        start = block * block_rows
        stop = start + block_rows
        low = 2 * (start // doc_rows * doc_rows)
        high = 2 * stop
        query_block = query_heads[start:stop]
        grad_block = grad_heads[start:stop]
        key_block = key_all[low:high]
        value_block = value_all[low:high]
        scores = (
            jnp.einsum("qhd,khd->hqk", query_block, key_block, preferred_element_type=jnp.float32)
            * scale
        )
        query_pos = 2 * (start + jnp.arange(block_rows, dtype=jnp.int32)) + parity
        key_pos = low + jnp.arange(high - low, dtype=jnp.int32)
        visible = key_pos[None, :] <= query_pos[:, None]
        scores = jnp.where(visible[None], scores, -jnp.inf)
        top = jnp.max(scores, axis=2, keepdims=True)
        weights = jnp.exp(scores - top)
        probs = weights / jnp.sum(weights, axis=2, keepdims=True)
        probs_low = probs.astype(jnp.bfloat16)
        dprob = jnp.einsum(
            "qhd,khd->hqk", grad_block, value_block, preferred_element_type=jnp.float32
        )
        delta = jnp.sum(probs * dprob, axis=2, keepdims=True)
        dscore = (probs * (dprob - delta) * scale).astype(jnp.bfloat16)
        query_parts.append(
            jnp.einsum(
                "hqk,khd->qhd", dscore, key_block, preferred_element_type=jnp.float32
            ).astype(jnp.bfloat16)
        )
        key_total = key_total.at[low:high].add(
            jnp.einsum("hqk,qhd->khd", dscore, query_block, preferred_element_type=jnp.float32)
        )
        value_total = value_total.at[low:high].add(
            jnp.einsum("hqk,qhd->khd", probs_low, grad_block, preferred_element_type=jnp.float32)
        )
    query_grad = jnp.concatenate(query_parts, axis=0).reshape(own_rows, group_width)

    def by_parity(total):
        paired = total.reshape(own_rows, 2, group_width)
        mine = jnp.where(is_even, paired[:, 0], paired[:, 1])
        theirs = jnp.where(is_even, paired[:, 1], paired[:, 0])
        return (mine.astype(jnp.bfloat16), theirs.astype(jnp.bfloat16))

    key_mine, key_theirs = by_parity(key_total)
    value_mine, value_theirs = by_parity(value_total)
    key_back, value_back = partner((key_theirs, value_theirs), "seq", 0)
    key_grad = (key_mine.astype(jnp.float32) + key_back.astype(jnp.float32)).astype(jnp.bfloat16)
    value_grad = (value_mine.astype(jnp.float32) + value_back.astype(jnp.float32)).astype(
        jnp.bfloat16
    )
    spread = jnp.broadcast_to(
        inputs[0].reshape(half_rows, 1, 2, model_width), (half_rows, groups, 2, model_width)
    ).reshape(half_rows, seq_count, model_width)
    input_rows = lax.all_to_all(spread, "seq", split_axis=1, concat_axis=0, tiled=True).reshape(
        own_rows, model_width
    )
    term = jnp.einsum("td,tc->dc", input_rows, value_grad, preferred_element_type=jnp.float32)
    halves = term.reshape(term.shape[0], 2, term.shape[1] // 2)
    mine = jnp.where(is_even, halves[:, 0], halves[:, 1])
    theirs = jnp.where(is_even, halves[:, 1], halves[:, 0])
    mine, theirs = (mine, theirs)
    received = partner(theirs.astype(jnp.bfloat16), "seq", 0).astype(theirs.dtype)
    weight_grad = lax.psum_scatter(
        (mine + received).astype(jnp.bfloat16), "dp", scatter_dimension=0, tiled=True
    ).astype(jnp.float32)

    def to_tokens(array):
        return array.reshape(seq_count, half_rows, 1, group_width)

    def from_heads(array):
        return (
            array.reshape(half_rows, groups, 2, group_width)
            .transpose(0, 2, 1, 3)
            .reshape(1, tok_rows, width)
        )

    returned = (
        lax.all_to_all(to_tokens(query_grad), "seq", split_axis=0, concat_axis=2, tiled=True),
        lax.all_to_all(to_tokens(key_grad), "seq", split_axis=0, concat_axis=2, tiled=True),
        lax.all_to_all(to_tokens(value_grad), "seq", split_axis=0, concat_axis=2, tiled=True),
    )
    return (from_heads(returned[0]), from_heads(returned[1]), from_heads(returned[2]), weight_grad)


def solution(mesh):
    return jax.shard_map(
        body,
        mesh=mesh,
        in_specs=(
            P("dp", "seq", None),
            P("dp", "seq", None),
            P("dp", "seq", None),
            P("dp", "seq", None),
            P("dp", "seq", None),
        ),
        out_specs=(
            P("dp", "seq", None),
            P("dp", "seq", None),
            P("dp", "seq", None),
            P("dp", "seq"),
        ),
        check_vma=False,
    )
```

profile of v0, /device:TPU:0, one launch (start us, length us, event | category | flops | bytes accessed | tf_op | source)
XLA Modules:
  0.0 255.6 jit_solution(17739342030090548654)
XLA Ops:
  9.6 6.5 %all-to-all-start.2 = ((bf16[64,8,512]{2,0,1:T(8,128)(2,1)}), bf16[64,8,512]{2,0,1:T(8,128)(2,1)S(1)}, u32[]{:S(2)}, u32[]{:S(2)}) async-start(bf16[64,8,512]{2,0,1:T(8,128)(2,1)} %bitcast.15), calls=%async_computation.2 | async-start | bytes 1048576 | tf_op jit(solution)/shard_map/all_to_all | solution.py:42
  17.4 14.0 %all-to-all-done.2 = bf16[64,8,512]{2,0,1:T(8,128)(2,1)S(1)} async-done(((bf16[64,8,512]{2,0,1:T(8,128)(2,1)}), bf16[64,8,512]{2,0,1:T(8,128)(2,1)S(1)}, u32[]{:S(2)}, u32[]{:S(2)}) %all-to-all-start.2) | async-done | bytes 524320 | tf_op jit(solution)/shard_map/all_to_all | solution.py:42
  31.4 3.6 %all-to-all-start.3 = ((bf16[64,8,512]{2,0,1:T(8,128)(2,1)}), bf16[64,8,512]{2,0,1:T(8,128)(2,1)S(1)}, u32[]{:S(2)}, u32[]{:S(2)}) async-start(bf16[64,8,512]{2,0,1:T(8,128)(2,1)} %bitcast.24), calls=%async_computation.3 | async-start | bytes 1048576 | tf_op jit(solution)/shard_map/all_to_all | solution.py:43
  36.4 13.9 %all-to-all-done.3 = bf16[64,8,512]{2,0,1:T(8,128)(2,1)S(1)} async-done(((bf16[64,8,512]{2,0,1:T(8,128)(2,1)}), bf16[64,8,512]{2,0,1:T(8,128)(2,1)S(1)}, u32[]{:S(2)}, u32[]{:S(2)}) %all-to-all-start.3) | async-done | bytes 524320 | tf_op jit(solution)/shard_map/all_to_all | solution.py:43
  50.4 3.5 %all-to-all-start = ((bf16[64,8,512]{2,0,1:T(8,128)(2,1)}), bf16[64,8,512]{2,0,1:T(8,128)(2,1)S(1)}, u32[]{:S(2)}, u32[]{:S(2)}) async-start(bf16[64,8,512]{2,0,1:T(8,128)(2,1)} %bitcast.1), calls=%async_computation | async-start | bytes 1048576 | tf_op jit(solution)/shard_map/all_to_all | solution.py:41
  55.9 13.2 %all-to-all-done = bf16[64,8,512]{2,0,1:T(8,128)(2,1)S(1)} async-done(((bf16[64,8,512]{2,0,1:T(8,128)(2,1)}), bf16[64,8,512]{2,0,1:T(8,128)(2,1)S(1)}, u32[]{:S(2)}, u32[]{:S(2)}) %all-to-all-start) | async-done | bytes 524320 | tf_op jit(solution)/shard_map/all_to_all | solution.py:41
  69.1 3.5 %all-to-all-start.1 = ((bf16[64,8,512]{2,0,1:T(8,128)(2,1)}), bf16[64,8,512]{2,0,1:T(8,128)(2,1)S(1)}, u32[]{:S(2)}, u32[]{:S(2)}) async-start(bf16[64,8,512]{2,0,1:T(8,128)(2,1)} %bitcast.10), calls=%async_computation.1 | async-start | bytes 1048576 | tf_op jit(solution)/shard_map/all_to_all | solution.py:40
  77.6 10.3 %all-to-all-done.1 = bf16[64,8,512]{2,0,1:T(8,128)(2,1)S(1)} async-done(((bf16[64,8,512]{2,0,1:T(8,128)(2,1)}), bf16[64,8,512]{2,0,1:T(8,128)(2,1)S(1)}, u32[]{:S(2)}, u32[]{:S(2)}) %all-to-all-start.1) | async-done | bytes 524320 | tf_op jit(solution)/shard_map/all_to_all | solution.py:40
  87.9 1.6 broadcast_in_dim.67
  89.5 3.8 %all-to-all-start.7 = ((bf16[64,8,2048]{2,0,1:T(8,128)(2,1)}), bf16[64,8,2048]{2,0,1:T(8,128)(2,1)S(1)}, u32[]{:S(2)}, u32[]{:S(2)}) async-start(bf16[64,8,2048]{2,0,1:T(8,128)(2,1)} %bitcast.65), calls=%async_computation.7 | async-start | bytes 4194304 | tf_op jit(solution)/shard_map/all_to_all | solution.py:118
  93.3 1.9 fusion.219
  96.8 1.6 slice.325
  100.7 1.6 slice.313
  110.2 2.1 fusion.236
  112.3 2.3 convolution_bitcast_fusion.3
  114.6 2.5 scatter-add.34
  117.1 2.1 fusion.221
  119.2 2.2 fusion.231
  121.4 2.4 fusion.17
  124.2 1.9 fusion.226
  126.1 2.4 fusion.24
  133.6 2.5 fusion.26
  136.2 3.9 %copy.167 = bf16[1024,4,128]{2,1,0:T(4,128)(2,1)} copy(f32[1024,4,128]{2,0,1:T(8,128)} %fusion.26) | data formatting | bytes 3145728 | tf_op jit(solution)/shard_map/scatter-add | solution.py:97
  141.6 3.0 %fusion.60 = (bf16[512,1,512]{2,1,0:T(2,128)(2,1)S(1)}, f32[512,1,512]{2,1,0:T(1,128)}) fusion(pred[]{:T(512)S(6)} %eq.5, bf16[512,2,512]{2,1,0:T(2,128)(2,1)S(1)} %reshape.498), kind=kLoop, calls=%fused_computation.98 | loop fusion | flops 786432 | bytes 2621441 | tf_op jit(solution)/shard_map/convert_element_type | solution.py:106
  146.0 2.4 fusion.54
  148.5 2.0 convolution_bitcast_fusion.9
  150.4 2.7 %fusion.53 = bf16[128,4,128]{2,0,1:T(8,128)(2,1)} fusion(f32[4,128,256]{1,2,0:T(8,128)} %convolution_bitcast_fusion.9, bf16[256,4,128]{2,1,0:T(4,128)(2,1)} %copy-done.18, f32[4,128,256]{1,2,0:T(8,128)} %get-tuple-element.129, f32[4,128]{1,0:T(4,128)S(1)} %get-tuple-element.128), kind=kOutput, calls=%fused_computation.91 | convolution fusion | flops 34538240 | bytes 1443840 | tf_op jit(solution)/shard_map/hqk,khd->qhd/dot_general | solution.py:90
  154.2 2.7 %fusion.52 = bf16[128,4,128]{2,0,1:T(8,128)(2,1)} fusion(f32[4,128,256]{1,2,0:T(8,128)} %convolution_bitcast_fusion.10, bf16[256,4,128]{2,1,0:T(4,128)(2,1)} %slice.311, f32[4,128,256]{1,2,0:T(8,128)} %get-tuple-element.131, f32[4,128]{1,0:T(4,128)S(1)} %get-tuple-element.130), kind=kOutput, calls=%fused_computation.90 | convolution fusion | flops 34538240 | bytes 1443840 | tf_op jit(solution)/shard_map/hqk,khd->qhd/dot_general | solution.py:90
  157.2 1.6 fusion.51
  160.3 2.4 convolution_bitcast_fusion.7
  162.7 2.6 %scatter-add.26 = f32[1024,4,128]{2,0,1:T(8,128)} pad(f32[256,4,128]{2,0,1:T(8,128)} %convolution_bitcast_fusion.7, f32[]{:T(128)} %constant.216.clone.1), padding=0_768x0_0x0_0 | pad | bytes 2621444 | tf_op jit(solution)/shard_map/scatter-add | solution.py:94
  165.3 2.8 %fusion.18 = f32[1024,4,128]{2,0,1:T(8,128)} fusion(f32[1024,4,128]{2,0,1:T(8,128)} %scatter-add.26, f32[4,128,256]{1,2,0:T(8,128)} %convolution_bitcast_fusion.10, bf16[128,4,128]{2,1,0:T(4,128)(2,1)S(1)} %copy-done.23, f32[4,128,256]{1,2,0:T(8,128)} %get-tuple-element.131, f32[4,128]{1,0:T(4,128)S(1)} %get-tuple-element.130), kind=kOutput, calls=%fused_computation.43 | convolution fusion | flops 34472704 | bytes 2756608 | tf_op jit(solution)/shard_map/hqk,qhd->khd/dot_general | solution.py:95
  168.1 2.1 fusion.62
  170.1 4.8 %all-to-all-start.4 = ((bf16[8,64,1,512]{3,1,2,0:T(8,128)(2,1)}), bf16[8,64,1,512]{3,1,2,0:T(8,128)(2,1)}, u32[]{:S(2)}, u32[]{:S(2)}) async-start(bf16[8,64,1,512]{3,1,2,0:T(8,128)(2,1)} %bitcast.239), calls=%async_computation.4 | async-start | bytes 1048576 | tf_op jit(solution)/shard_map/all_to_all | solution.py:142
  174.9 2.3 fusion.241
  177.3 2.2 fusion.218
  179.5 1.9 copy.182
  181.4 2.9 %copy.181 = f32[2048,1,256]{2,0,1:T(8,128)} copy(f32[2048,1,256]{0,2,1:T(8,128)} %get-tuple-element.100) | data formatting | bytes 4194304
  185.6 2.1 collective-permute-start.4
  187.7 2.8 %fusion.20 = f32[1024,4,128]{2,0,1:T(8,128)} fusion(f32[1024,4,128]{2,0,1:T(8,128)} %fusion.18, f32[4,128,256]{1,2,0:T(8,128)} %convolution_bitcast_fusion.9, bf16[128,4,128]{2,1,0:T(4,128)(2,1)S(1)} %copy-done.22, f32[4,128,256]{1,2,0:T(8,128)} %get-tuple-element.129, f32[4,128]{1,0:T(4,128)S(1)} %get-tuple-element.128), kind=kOutput, calls=%fused_computation.50 | convolution fusion | flops 34603776 | bytes 3280896 | tf_op jit(solution)/shard_map/hqk,qhd->khd/dot_general | solution.py:95
  190.5 2.8 %fusion.22 = f32[1024,4,128]{2,0,1:T(8,128)} fusion(f32[1024,4,128]{2,0,1:T(8,128)} %fusion.20, f32[4,128,256]{1,2,0:T(8,128)} %copy-done.7, bf16[128,4,128]{2,1,0:T(4,128)(2,1)S(1)} %copy-done.20, f32[4,128,256]{1,2,0:T(8,128)} %get-tuple-element.127, f32[4,128]{1,0:T(4,128)S(1)} %get-tuple-element.126), kind=kOutput, calls=%fused_computation.52 | convolution fusion | flops 34603776 | bytes 3280896 | tf_op jit(solution)/shard_map/hqk,qhd->khd/dot_general | solution.py:95
  193.3 3.9 %copy.160 = bf16[1024,4,128]{2,1,0:T(4,128)(2,1)} copy(f32[1024,4,128]{2,0,1:T(8,128)} %fusion.22) | data formatting | bytes 3145728 | tf_op jit(solution)/shard_map/scatter-add | solution.py:94
  198.7 3.0 %fusion.57 = (bf16[512,1,512]{2,1,0:T(2,128)(2,1)S(1)}, f32[512,1,512]{2,1,0:T(1,128)}) fusion(pred[]{:T(512)S(6)} %eq.5, bf16[512,2,512]{2,1,0:T(2,128)(2,1)S(1)} %reshape.494), kind=kLoop, calls=%fused_computation.95 | loop fusion | flops 786432 | bytes 2621441 | tf_op jit(solution)/shard_map/convert_element_type | solution.py:106
  202.7 2.7 %fusion.8 = bf16[2048,256]{1,0:T(8,128)(2,1)} fusion(bf16[2048,256]{1,0:T(8,128)(2,1)} %collective-permute-done.4, f32[2048,1,256]{2,0,1:T(8,128)S(1)} %copy-done, f32[2048,1,256]{2,0,1:T(8,128)S(1)} %copy.182, pred[]{:T(512)S(6)} %eq.5), kind=kLoop, calls=%fused_computation.9 | loop fusion | flops 2097152 | bytes 6291457 | tf_op jit(solution)/shard_map/convert_element_type | solution.py:128
  206.7 19.9 %all_to_all.120 = bf16[8,64,1,512]{3,1,2,0:T(8,128)(2,1)S(1)} all-to-all(bf16[8,64,1,512]{3,1,2,0:T(8,128)(2,1)S(1)} %bitcast.248), channel_id=1, replica_groups=mesh['dp'=4,'seq'=8] {'seq'}, dimensions={0} | all-to-all | bytes 1048576 | tf_op jit(solution)/shard_map/all_to_all | solution.py:143
  226.6 3.8 %all-to-all-start.6 = ((bf16[8,64,1,512]{3,1,2,0:T(8,128)(2,1)}), bf16[8,64,1,512]{3,1,2,0:T(8,128)(2,1)S(1)}, u32[]{:S(2)}, u32[]{:S(2)}) async-start(bf16[8,64,1,512]{3,1,2,0:T(8,128)(2,1)} %bitcast.60), calls=%async_computation.6 | async-start | bytes 1048576 | tf_op jit(solution)/shard_map/all_to_all | solution.py:144
  234.6 10.8 %all-to-all-done.6 = bf16[8,64,1,512]{3,1,2,0:T(8,128)(2,1)S(1)} async-done(((bf16[8,64,1,512]{3,1,2,0:T(8,128)(2,1)}), bf16[8,64,1,512]{3,1,2,0:T(8,128)(2,1)S(1)}, u32[]{:S(2)}, u32[]{:S(2)}) %all-to-all-start.6) | async-done | bytes 524320 | tf_op jit(solution)/shard_map/all_to_all | solution.py:144
  247.0 1.8 convert_element_type.141
  (134 shorter events, 45.7 us)
Async XLA Ops:
  7.2 8.9 %copy-start.12 = (bf16[1,128,2048]{2,1,0:T(8,128)(2,1)S(1)}, bf16[1,128,2048]{2,1,0:T(8,128)(2,1)}, u32[]{:S(2)}) copy-start(bf16[1,128,2048]{2,1,0:T(8,128)(2,1)} %param.24) | copy-start | bytes 1572868
  9.6 25.5 %copy-start.13 = (bf16[1,128,2048]{2,1,0:T(8,128)(2,1)S(1)}, bf16[1,128,2048]{2,1,0:T(8,128)(2,1)}, u32[]{:S(2)}) copy-start(bf16[1,128,2048]{2,1,0:T(8,128)(2,1)} %param.22) | copy-start | bytes 1572868
  9.6 21.8 %all-to-all-start.2 = ((bf16[64,8,512]{2,0,1:T(8,128)(2,1)}), bf16[64,8,512]{2,0,1:T(8,128)(2,1)S(1)}, u32[]{:S(2)}, u32[]{:S(2)}) async-start(bf16[64,8,512]{2,0,1:T(8,128)(2,1)} %bitcast.15), calls=%async_computation.2 | async-start | bytes 1048576 | tf_op jit(solution)/shard_map/all_to_all | solution.py:42
  31.4 22.4 %copy-start.14 = (bf16[1,128,2048]{2,1,0:T(8,128)(2,1)S(1)}, bf16[1,128,2048]{2,1,0:T(8,128)(2,1)}, u32[]{:S(2)}) copy-start(bf16[1,128,2048]{2,1,0:T(8,128)(2,1)} %param.21) | copy-start | bytes 1572868
  31.4 18.9 %all-to-all-start.3 = ((bf16[64,8,512]{2,0,1:T(8,128)(2,1)}), bf16[64,8,512]{2,0,1:T(8,128)(2,1)S(1)}, u32[]{:S(2)}, u32[]{:S(2)}) async-start(bf16[64,8,512]{2,0,1:T(8,128)(2,1)} %bitcast.24), calls=%async_computation.3 | async-start | bytes 1048576 | tf_op jit(solution)/shard_map/all_to_all | solution.py:43
  50.4 18.8 %all-to-all-start = ((bf16[64,8,512]{2,0,1:T(8,128)(2,1)}), bf16[64,8,512]{2,0,1:T(8,128)(2,1)S(1)}, u32[]{:S(2)}, u32[]{:S(2)}) async-start(bf16[64,8,512]{2,0,1:T(8,128)(2,1)} %bitcast.1), calls=%async_computation | async-start | bytes 1048576 | tf_op jit(solution)/shard_map/all_to_all | solution.py:41
  69.1 18.8 %all-to-all-start.1 = ((bf16[64,8,512]{2,0,1:T(8,128)(2,1)}), bf16[64,8,512]{2,0,1:T(8,128)(2,1)S(1)}, u32[]{:S(2)}, u32[]{:S(2)}) async-start(bf16[64,8,512]{2,0,1:T(8,128)(2,1)} %bitcast.10), calls=%async_computation.1 | async-start | bytes 1048576 | tf_op jit(solution)/shard_map/all_to_all | solution.py:40
  74.1 30.5 %collective-permute-start = (bf16[512,512]{1,0:T(8,128)(2,1)S(1)}, bf16[512,512]{1,0:T(8,128)(2,1)}, u32[]{:S(2)}, u32[]{:S(2)}) collective-permute-start(bf16[512,512]{1,0:T(8,128)(2,1)S(1)} %bitcast.238), channel_id=1, source_target_pairs={{0,1},{1,0},{2,3},{3,2},{4,5},{5,4},{6,7},{7,6},{8,9},{9,8},{10,11... | collective-permute-start | bytes 1572872 | tf_op jit(solution)/shard_map/ppermute | solution.py:10
  76.6 51.8 %collective-permute-start.1 = (bf16[512,512]{1,0:T(8,128)(2,1)S(1)}, bf16[512,512]{1,0:T(8,128)(2,1)}, u32[]{:S(2)}, u32[]{:S(2)}) collective-permute-start(bf16[512,512]{1,0:T(8,128)(2,1)S(1)} %bitcast.237), channel_id=1, source_target_pairs={{0,1},{1,0},{2,3},{3,2},{4,5},{5,4},{6,7},{7,6},{8,9},{9,8},{10,11... | collective-permute-start | bytes 1572872 | tf_op jit(solution)/shard_map/ppermute | solution.py:10
  87.9 1.6 copy-start.3
  89.5 80.6 %all-to-all-start.7 = ((bf16[64,8,2048]{2,0,1:T(8,128)(2,1)}), bf16[64,8,2048]{2,0,1:T(8,128)(2,1)S(1)}, u32[]{:S(2)}, u32[]{:S(2)}) async-start(bf16[64,8,2048]{2,0,1:T(8,128)(2,1)} %bitcast.65), calls=%async_computation.7 | async-start | bytes 4194304 | tf_op jit(solution)/shard_map/all_to_all | solution.py:118
  110.1 6.9 %copy-start.15 = (bf16[256,4,128]{2,1,0:T(4,128)(2,1)}, bf16[256,4,128]{2,1,0:T(4,128)(2,1)S(1)}, u32[]{:S(2)}) copy-start(bf16[256,4,128]{2,1,0:T(4,128)(2,1)S(1)} %slice.303) | copy-start | bytes 786436
  112.3 4.8 %copy-start.19 = (bf16[128,4,128]{2,1,0:T(4,128)(2,1)S(1)}, bf16[128,4,128]{2,1,0:T(4,128)(2,1)}, u32[]{:S(2)}) copy-start(bf16[128,4,128]{2,1,0:T(4,128)(2,1)} %slice.329) | copy-start | bytes 393220
  117.1 4.3 %copy-start.9 = (bf16[128,4,128]{2,1,0:T(4,128)(2,1)S(1)}, bf16[128,4,128]{2,1,0:T(4,128)(2,1)}, u32[]{:S(2)}) copy-start(bf16[128,4,128]{2,1,0:T(4,128)(2,1)} %slice.317) | copy-start | bytes 393220
  121.4 2.8 %copy-start.21 = (bf16[128,4,128]{2,1,0:T(4,128)(2,1)S(1)}, bf16[128,4,128]{2,1,0:T(4,128)(2,1)}, u32[]{:S(2)}) copy-start(bf16[128,4,128]{2,1,0:T(4,128)(2,1)} %slice.321) | copy-start | bytes 393220
  121.4 4.7 %copy-start.11 = (bf16[128,4,128]{2,1,0:T(4,128)(2,1)S(1)}, bf16[128,4,128]{2,1,0:T(4,128)(2,1)}, u32[]{:S(2)}) copy-start(bf16[128,4,128]{2,1,0:T(4,128)(2,1)} %slice.325) | copy-start | bytes 393220
  124.2 4.3 %copy-start.18 = (bf16[256,4,128]{2,1,0:T(4,128)(2,1)}, bf16[256,4,128]{2,1,0:T(4,128)(2,1)S(1)}, u32[]{:S(2)}) copy-start(bf16[256,4,128]{2,1,0:T(4,128)(2,1)S(1)} %slice.319) | copy-start | bytes 786436
  141.5 4.2 %copy-start.6 = (bf16[256,4,128]{2,1,0:T(4,128)(2,1)S(1)}, bf16[256,4,128]{2,1,0:T(4,128)(2,1)}, u32[]{:S(2)}) copy-start(bf16[256,4,128]{2,1,0:T(4,128)(2,1)} %slice.331) | copy-start | bytes 786436
  144.6 1.4 copy-start.17
  145.5 2.9 %copy-start.5 = (bf16[256,4,128]{2,1,0:T(4,128)(2,1)S(1)}, bf16[256,4,128]{2,1,0:T(4,128)(2,1)}, u32[]{:S(2)}) copy-start(bf16[256,4,128]{2,1,0:T(4,128)(2,1)} %slice.323) | copy-start | bytes 786436
  145.5 22.5 %collective-permute-start.3 = (bf16[512,512]{1,0:T(8,128)(2,1)}, bf16[512,512]{1,0:T(8,128)(2,1)}, u32[]{:S(2)}, u32[]{:S(2)}) collective-permute-start(bf16[512,512]{1,0:T(8,128)(2,1)} %bitcast.233), channel_id=1, source_target_pairs={{0,1},{1,0},{2,3},{3,2},{4,5},{5,4},{6,7},{7,6},{8,9},{9,8},{10,11... | collective-permute-start | bytes 1572872 | tf_op jit(solution)/shard_map/ppermute | solution.py:10
  146.0 7.2 %copy-start.7 = (f32[4,128,256]{1,2,0:T(8,128)}, f32[4,128,256]{1,2,0:T(8,128)S(1)}, u32[]{:S(2)}) copy-start(f32[4,128,256]{1,2,0:T(8,128)S(1)} %convolution_bitcast_fusion.8) | copy-start | bytes 1572868
  148.5 4.7 %copy-start.4 = (bf16[256,4,128]{2,1,0:T(4,128)(2,1)S(1)}, bf16[256,4,128]{2,1,0:T(4,128)(2,1)}, u32[]{:S(2)}) copy-start(bf16[256,4,128]{2,1,0:T(4,128)(2,1)} %slice.315) | copy-start | bytes 786436
  148.5 4.7 %copy-start.10 = (bf16[128,4,128]{2,1,0:T(4,128)(2,1)S(1)}, bf16[128,4,128]{2,1,0:T(4,128)(2,1)}, u32[]{:S(2)}) copy-start(bf16[128,4,128]{2,1,0:T(4,128)(2,1)} %slice.317) | copy-start | bytes 393220
  153.2 3.8 %copy-start.8 = (bf16[128,4,128]{2,1,0:T(4,128)(2,1)S(1)}, bf16[128,4,128]{2,1,0:T(4,128)(2,1)}, u32[]{:S(2)}) copy-start(bf16[128,4,128]{2,1,0:T(4,128)(2,1)} %slice.309) | copy-start | bytes 393220
  154.2 3.0 %copy-start.16 = (bf16[256,4,128]{2,1,0:T(4,128)(2,1)S(1)}, bf16[256,4,128]{2,1,0:T(4,128)(2,1)}, u32[]{:S(2)}) copy-start(bf16[256,4,128]{2,1,0:T(4,128)(2,1)} %copy-done.15) | copy-start | bytes 786436
  156.9 1.9 copy-start.25
  157.0 1.9 copy-start.26
  157.2 1.7 copy-start.27
  158.9 1.5 copy-start.24
  160.3 5.0 %copy-start.23 = (bf16[128,4,128]{2,1,0:T(4,128)(2,1)S(1)}, bf16[128,4,128]{2,1,0:T(4,128)(2,1)}, u32[]{:S(2)}) copy-start(bf16[128,4,128]{2,1,0:T(4,128)(2,1)} %slice.313) | copy-start | bytes 393220
  162.7 5.4 %copy-start.1 = (f32[512,1,512]{2,1,0:T(1,128)S(1)}, f32[512,1,512]{2,1,0:T(1,128)}, u32[]{:S(2)}) copy-start(f32[512,1,512]{2,1,0:T(1,128)} %get-tuple-element.103) | copy-start | bytes 3145732
  170.1 36.5 %all-to-all-start.4 = ((bf16[8,64,1,512]{3,1,2,0:T(8,128)(2,1)}), bf16[8,64,1,512]{3,1,2,0:T(8,128)(2,1)}, u32[]{:S(2)}, u32[]{:S(2)}) async-start(bf16[8,64,1,512]{3,1,2,0:T(8,128)(2,1)} %bitcast.239), calls=%async_computation.4 | async-start | bytes 1048576 | tf_op jit(solution)/shard_map/all_to_all | solution.py:142
  174.9 72.1 %reduce-scatter.2.cloned.1.call-start = ((), (), s32[]{:S(2)}) async-start(), calls=%async_computation.9 | async-start | bytes 1310720 | tf_op jit(solution)/shard_map/reduce_scatter | solution.py:127
  184.4 3.3 %copy-start.22 = (bf16[128,4,128]{2,1,0:T(4,128)(2,1)S(1)}, bf16[128,4,128]{2,1,0:T(4,128)(2,1)}, u32[]{:S(2)}) copy-start(bf16[128,4,128]{2,1,0:T(4,128)(2,1)} %slice.321) | copy-start | bytes 393220
  185.6 4.9 %copy-start.20 = (bf16[128,4,128]{2,1,0:T(4,128)(2,1)S(1)}, bf16[128,4,128]{2,1,0:T(4,128)(2,1)}, u32[]{:S(2)}) copy-start(bf16[128,4,128]{2,1,0:T(4,128)(2,1)} %slice.329) | copy-start | bytes 393220
  185.6 17.1 %collective-permute-start.4 = (bf16[2048,256]{1,0:T(8,128)(2,1)}, bf16[2048,256]{1,0:T(8,128)(2,1)}, u32[]{:S(2)}, u32[]{:S(2)}) collective-permute-start(bf16[2048,256]{1,0:T(8,128)(2,1)} %fusion.61), channel_id=1, source_target_pairs={{0,1},{1,0},{2,3},{3,2},{4,5},{5,4},{6,7},{7,6},{8,9},{9,8},{10,11... | collective-permute-start | bytes 3145736 | tf_op jit(solution)/shard_map/ppermute | solution.py:10
  198.7 3.9 %copy-start = (f32[2048,1,256]{2,0,1:T(8,128)S(1)}, f32[2048,1,256]{2,0,1:T(8,128)}, u32[]{:S(2)}) copy-start(f32[2048,1,256]{2,0,1:T(8,128)} %copy.181) | copy-start | bytes 6291460
  202.7 2.8 %copy-start.2 = (f32[512,1,512]{2,1,0:T(1,128)S(1)}, f32[512,1,512]{2,1,0:T(1,128)}, u32[]{:S(2)}) copy-start(f32[512,1,512]{2,1,0:T(1,128)} %get-tuple-element.105) | copy-start | bytes 3145732
  202.7 2.8 %collective-permute-start.2 = (bf16[512,512]{1,0:T(8,128)(2,1)}, bf16[512,512]{1,0:T(8,128)(2,1)}, u32[]{:S(2)}, u32[]{:S(2)}) collective-permute-start(bf16[512,512]{1,0:T(8,128)(2,1)} %bitcast.234), channel_id=1, source_target_pairs={{0,1},{1,0},{2,3},{3,2},{4,5},{5,4},{6,7},{7,6},{8,9},{9,8},{10,11... | collective-permute-start | bytes 1572872 | tf_op jit(solution)/shard_map/ppermute | solution.py:10
  226.6 18.8 %all-to-all-start.6 = ((bf16[8,64,1,512]{3,1,2,0:T(8,128)(2,1)}), bf16[8,64,1,512]{3,1,2,0:T(8,128)(2,1)S(1)}, u32[]{:S(2)}, u32[]{:S(2)}) async-start(bf16[8,64,1,512]{3,1,2,0:T(8,128)(2,1)} %bitcast.60), calls=%async_computation.6 | async-start | bytes 1048576 | tf_op jit(solution)/shard_map/all_to_all | solution.py:144
Sparse Core Ops, SparseCore 0:
  205.5 28.9 reduce-scatter.1
where the time goes:
time: 258 us; the launch traced here: 256 us
  waiting for transfers between devices  62.4 us (24%)
  local copies, waits for them, and re-layouts  61.6 us (24%)
  matrix products  44 us (17%)
  starting transfers between devices  32.3 us (13%)
  other arithmetic  21 us (8%)
  blocking collectives  19.9 us (8%)
  between operations  14.5 us (6%)
    all_to_all x1, blocking collectives, body(): lax.all_to_all(to_tokens(key_grad), 'seq', split_axis=0, concat_axis=2, t...  19.9 us
    all_to_all x1, waiting for transfers between devices, body(): lax.all_to_all(to_heads(values), 'seq', split_axis=1, concat_axis=0, tile...  14 us
    all_to_all x1, waiting for transfers between devices, body(): lax.all_to_all(to_heads(out_grad), 'seq', split_axis=1, concat_axis=0, ti...  13.9 us
    all_to_all x1, waiting for transfers between devices, body(): lax.all_to_all(to_heads(key_vectors), 'seq', split_axis=1, concat_axis=0,...  13.2 us
    dot_general x4, matrix products, body(): jnp.einsum('hqk,qhd->khd', dscore, query_block, preferred_element_type=jn...  10.8 us
    all_to_all x1, waiting for transfers between devices, body(): lax.all_to_all(to_tokens(value_grad), 'seq', split_axis=0, concat_axis=2,...  10.8 us
    all_to_all x1, waiting for transfers between devices, body(): lax.all_to_all(to_heads(queries), 'seq', split_axis=1, concat_axis=0, til...  10.3 us
    dot_general x4, matrix products, body(): jnp.einsum('hqk,qhd->khd', probs_low, grad_block, preferred_element_type=...  9.58 us
  transfers between devices with their start and end apart: 13, of which 5 were waited for; matrix products, arithmetic and copies ran while one was open for 48% of the time, Pallas kernels for 0%

commit v1 on v0

--- a/solution.py
+++ b/solution.py
@@ -4,6 +4,28 @@
 from jax.sharding import PartitionSpec as P
 
 HD = 128
+
+
+def in_blocks(x, dim, size):
+    before, after = (x.shape[:dim], x.shape[dim + 1 :])
+    return jnp.moveaxis(x.reshape(*before, size, -1, *after), dim, 0)
+
+
+def laid_out(tiles, dim):
+    shape = list(tiles.shape[1:])
+    shape[dim] *= tiles.shape[0]
+    return jnp.moveaxis(tiles, 0, dim).reshape(shape)
+
+
+def pairwise_exchange(x, axis, split_dim, concat_dim):
+    size, here = (lax.axis_size(axis), lax.axis_index(axis))
+    pieces = in_blocks(x, split_dim, size)
+    outs = [pieces[here]]
+    for step in range(1, size):
+        sent = pieces[here ^ step]
+        outs.append(lax.ppermute(sent, axis, [(i, i ^ step) for i in range(size)]))
+    pieces = jnp.stack(outs)[here ^ jnp.arange(size)]
+    return laid_out(pieces, concat_dim)
 
 
 def partner(value, axis, apart):
@@ -141,7 +163,7 @@
     returned = (
         lax.all_to_all(to_tokens(query_grad), "seq", split_axis=0, concat_axis=2, tiled=True),
         lax.all_to_all(to_tokens(key_grad), "seq", split_axis=0, concat_axis=2, tiled=True),
-        lax.all_to_all(to_tokens(value_grad), "seq", split_axis=0, concat_axis=2, tiled=True),
+        pairwise_exchange(to_tokens(value_grad), "seq", 0, 2),
     )
     return (from_heads(returned[0]), from_heads(returned[1]), from_heads(returned[2]), weight_grad)
 

time: 258 us -> 247 us (0.957)
  blocking collectives: 19.9 us -> 0 us
  starting transfers between devices: 32.3 us -> 42 us
    all_to_all x1 -> x0, blocking collectives: 19.9 us -> none  [body(): lax.all_to_all(to_tokens(key_grad), 'seq', split_axis=0, concat_axis=2, t...]
    ppermute x0 -> x7, starting transfers between devices: none -> 8.44 us  [pairwise_exchange(): outs.append(lax.ppermute(sent, axis, [(i, i ^ step) for i in range(size)]))]
    unnamed x60 -> x70, local copies, waits for them, and re-layouts: 6.83 us -> 5.24 us
  transfers between devices with their start and end apart: 13 -> 20, of which waited for: 5 -> 6; matrix products, arithmetic and copies ran while one was open for 48% -> 50% of each run, Pallas kernels for 0% -> 0%
where the time goes in v1:
time: 247 us; the launch traced here: 245 us
  waiting for transfers between devices  61.9 us (25%)
  local copies, waits for them, and re-layouts  59.5 us (24%)
  matrix products  44.2 us (18%)
  starting transfers between devices  42 us (17%)
  other arithmetic  22.3 us (9%)
  between operations  14.6 us (6%)
    all_to_all x1, waiting for transfers between devices, body(): lax.all_to_all(to_heads(values), 'seq', split_axis=1, concat_axis=0, tile...  14 us
    all_to_all x1, waiting for transfers between devices, body(): lax.all_to_all(to_heads(out_grad), 'seq', split_axis=1, concat_axis=0, ti...  13.9 us
    all_to_all x1, waiting for transfers between devices, body(): lax.all_to_all(to_heads(key_vectors), 'seq', split_axis=1, concat_axis=0,...  12.6 us
    all_to_all x1, waiting for transfers between devices, body(): lax.all_to_all(to_heads(queries), 'seq', split_axis=1, concat_axis=0, til...  10.9 us
    dot_general x4, matrix products, body(): jnp.einsum('hqk,khd->qhd', dscore, key_block, preferred_element_type=jnp....  10.4 us
    dot_general x4, matrix products, body(): jnp.einsum('hqk,qhd->khd', dscore, query_block, preferred_element_type=jn...  10.4 us
    dot_general x4, matrix products, body(): jnp.einsum('hqk,qhd->khd', probs_low, grad_block, preferred_element_type=...  9.57 us
    all_to_all x1, waiting for transfers between devices, body(): lax.all_to_all(to_tokens(key_grad), 'seq', split_axis=0, concat_axis=2, t...  9.14 us
  transfers between devices with their start and end apart: 20, of which 6 were waited for; matrix products, arithmetic and copies ran while one was open for 50% of the time, Pallas kernels for 0%

profile of v1, /device:TPU:0, one launch (start us, length us, event | category | flops | bytes accessed | tf_op | source)
XLA Modules:
  0.0 244.6 jit_solution(12995271659172889130)
XLA Ops:
  9.6 6.5 %all-to-all-start.2 = ((bf16[64,8,512]{2,0,1:T(8,128)(2,1)}), bf16[64,8,512]{2,0,1:T(8,128)(2,1)S(1)}, u32[]{:S(2)}, u32[]{:S(2)}) async-start(bf16[64,8,512]{2,0,1:T(8,128)(2,1)} %bitcast.15), calls=%async_computation.2 | async-start | bytes 1048576 | tf_op jit(solution)/shard_map/all_to_all | solution.py:64
  17.4 14.0 %all-to-all-done.2 = bf16[64,8,512]{2,0,1:T(8,128)(2,1)S(1)} async-done(((bf16[64,8,512]{2,0,1:T(8,128)(2,1)}), bf16[64,8,512]{2,0,1:T(8,128)(2,1)S(1)}, u32[]{:S(2)}, u32[]{:S(2)}) %all-to-all-start.2) | async-done | bytes 524320 | tf_op jit(solution)/shard_map/all_to_all | solution.py:64
  31.4 3.6 %all-to-all-start.3 = ((bf16[64,8,512]{2,0,1:T(8,128)(2,1)}), bf16[64,8,512]{2,0,1:T(8,128)(2,1)S(1)}, u32[]{:S(2)}, u32[]{:S(2)}) async-start(bf16[64,8,512]{2,0,1:T(8,128)(2,1)} %bitcast.24), calls=%async_computation.3 | async-start | bytes 1048576 | tf_op jit(solution)/shard_map/all_to_all | solution.py:65
  36.4 13.9 %all-to-all-done.3 = bf16[64,8,512]{2,0,1:T(8,128)(2,1)S(1)} async-done(((bf16[64,8,512]{2,0,1:T(8,128)(2,1)}), bf16[64,8,512]{2,0,1:T(8,128)(2,1)S(1)}, u32[]{:S(2)}, u32[]{:S(2)}) %all-to-all-start.3) | async-done | bytes 524320 | tf_op jit(solution)/shard_map/all_to_all | solution.py:65
  50.4 3.5 %all-to-all-start = ((bf16[64,8,512]{2,0,1:T(8,128)(2,1)}), bf16[64,8,512]{2,0,1:T(8,128)(2,1)S(1)}, u32[]{:S(2)}, u32[]{:S(2)}) async-start(bf16[64,8,512]{2,0,1:T(8,128)(2,1)} %bitcast.1), calls=%async_computation | async-start | bytes 1048576 | tf_op jit(solution)/shard_map/all_to_all | solution.py:63
  56.6 12.6 %all-to-all-done = bf16[64,8,512]{2,0,1:T(8,128)(2,1)S(1)} async-done(((bf16[64,8,512]{2,0,1:T(8,128)(2,1)}), bf16[64,8,512]{2,0,1:T(8,128)(2,1)S(1)}, u32[]{:S(2)}, u32[]{:S(2)}) %all-to-all-start) | async-done | bytes 524320 | tf_op jit(solution)/shard_map/all_to_all | solution.py:63
  69.1 3.5 %all-to-all-start.1 = ((bf16[64,8,512]{2,0,1:T(8,128)(2,1)}), bf16[64,8,512]{2,0,1:T(8,128)(2,1)S(1)}, u32[]{:S(2)}, u32[]{:S(2)}) async-start(bf16[64,8,512]{2,0,1:T(8,128)(2,1)} %bitcast.10), calls=%async_computation.1 | async-start | bytes 1048576 | tf_op jit(solution)/shard_map/all_to_all | solution.py:62
  77.0 10.9 %all-to-all-done.1 = bf16[64,8,512]{2,0,1:T(8,128)(2,1)S(1)} async-done(((bf16[64,8,512]{2,0,1:T(8,128)(2,1)}), bf16[64,8,512]{2,0,1:T(8,128)(2,1)S(1)}, u32[]{:S(2)}, u32[]{:S(2)}) %all-to-all-start.1) | async-done | bytes 524320 | tf_op jit(solution)/shard_map/all_to_all | solution.py:62
  87.9 1.6 broadcast_in_dim.68
  89.5 3.8 %all-to-all-start.6 = ((bf16[64,8,2048]{2,0,1:T(8,128)(2,1)}), bf16[64,8,2048]{2,0,1:T(8,128)(2,1)S(1)}, u32[]{:S(2)}, u32[]{:S(2)}) async-start(bf16[64,8,2048]{2,0,1:T(8,128)(2,1)} %bitcast.80), calls=%async_computation.6 | async-start | bytes 4194304 | tf_op jit(solution)/shard_map/all_to_all | solution.py:140
  93.3 1.9 fusion.220
  96.8 1.6 slice.325
  100.7 1.6 slice.313
  110.2 2.1 fusion.237
  112.3 2.3 convolution_bitcast_fusion.3
  114.6 2.5 %scatter-add.34 = f32[1024,4,128]{2,0,1:T(8,128)} pad(f32[256,4,128]{2,0,1:T(8,128)} %convolution_bitcast_fusion.3, f32[]{:T(128)} %constant.225.clone.1), padding=0_768x0_0x0_0 | pad | bytes 2621444 | tf_op jit(solution)/shard_map/scatter-add | solution.py:119
  117.1 2.1 fusion.222
  119.2 2.2 fusion.232
  121.4 2.4 fusion.17
  124.3 1.9 fusion.227
  126.2 2.4 fusion.24
  133.7 2.5 %fusion.26 = f32[1024,4,128]{2,0,1:T(8,128)} fusion(f32[1024,4,128]{2,0,1:T(8,128)} %fusion.24, bf16[128,4,128]{2,1,0:T(4,128)(2,1)S(1)} %slice.333, f32[4,128]{1,0:T(4,128)S(1)} %get-tuple-element.134, pred[128,256]{0,1:T(8,128)(4,1)} %broadcast_compare_fusion, bf16[256,4,128]{2,1,0:T(4,128)(2,1)} %slice.327, bf16[128,4,128]{2,1,0:T(4,128)(2,1)} %slice.329), kind=kOutput, calls=%fused_computation.57 | convolution fusion | flops 67896064 | bytes 1607680 | tf_op jit(solution)/shard_map/hqk,qhd->khd/dot_general | solution.py:120
  136.2 3.9 %copy.167 = bf16[1024,4,128]{2,1,0:T(4,128)(2,1)} copy(f32[1024,4,128]{2,0,1:T(8,128)} %fusion.26) | data formatting | bytes 3145728 | tf_op jit(solution)/shard_map/scatter-add | solution.py:119
  141.6 3.0 %fusion.60 = (bf16[512,1,512]{2,1,0:T(2,128)(2,1)S(1)}, f32[512,1,512]{2,1,0:T(1,128)}) fusion(pred[]{:T(512)S(6)} %eq.5, bf16[512,2,512]{2,1,0:T(2,128)(2,1)S(1)} %reshape.507), kind=kLoop, calls=%fused_computation.99 | loop fusion | flops 786432 | bytes 2621441 | tf_op jit(solution)/shard_map/convert_element_type | solution.py:128
  146.1 2.6 %fusion.54 = bf16[128,4,128]{2,0,1:T(8,128)(2,1)} fusion(f32[4,128,256]{1,2,0:T(8,128)} %convolution_bitcast_fusion.8, bf16[256,4,128]{2,1,0:T(4,128)(2,1)S(1)} %copy-done.17, f32[4,128,256]{1,2,0:T(8,128)} %get-tuple-element.135, f32[4,128]{1,0:T(4,128)S(1)} %get-tuple-element.134), kind=kOutput, calls=%fused_computation.93 | convolution fusion | flops 34538240 | bytes 1443840 | tf_op jit(solution)/shard_map/hqk,khd->qhd/dot_general | solution.py:112
  148.7 2.0 convolution_bitcast_fusion.9
  150.7 2.7 %fusion.53 = bf16[128,4,128]{2,0,1:T(8,128)(2,1)} fusion(f32[4,128,256]{1,2,0:T(8,128)} %convolution_bitcast_fusion.9, bf16[256,4,128]{2,1,0:T(4,128)(2,1)} %copy-done.18, f32[4,128,256]{1,2,0:T(8,128)} %get-tuple-element.137, f32[4,128]{1,0:T(4,128)S(1)} %get-tuple-element.136), kind=kOutput, calls=%fused_computation.92 | convolution fusion | flops 34538240 | bytes 1443840 | tf_op jit(solution)/shard_map/hqk,khd->qhd/dot_general | solution.py:112
  154.4 2.6 %fusion.52 = bf16[128,4,128]{2,0,1:T(8,128)(2,1)} fusion(f32[4,128,256]{1,2,0:T(8,128)} %convolution_bitcast_fusion.10, bf16[256,4,128]{2,1,0:T(4,128)(2,1)} %slice.311, f32[4,128,256]{1,2,0:T(8,128)} %get-tuple-element.139, f32[4,128]{1,0:T(4,128)S(1)} %copy-done.28), kind=kOutput, calls=%fused_computation.91 | convolution fusion | flops 34538240 | bytes 1443840 | tf_op jit(solution)/shard_map/hqk,khd->qhd/dot_general | solution.py:112
  157.3 2.5 %fusion.51 = bf16[128,4,128]{2,0,1:T(8,128)(2,1)} fusion(f32[4,128,256]{1,2,0:T(8,128)S(1)} %convolution_bitcast_fusion.11, bf16[256,4,128]{2,1,0:T(4,128)(2,1)} %copy-done.16, f32[4,128,256]{1,2,0:T(8,128)} %get-tuple-element.141, f32[4,128]{1,0:T(4,128)S(1)} %get-tuple-element.140), kind=kOutput, calls=%fused_computation.90 | convolution fusion | flops 34538240 | bytes 1443840 | tf_op jit(solution)/shard_map/hqk,khd->qhd/dot_general | solution.py:112
  162.3 2.0 convolution_bitcast_fusion.7
  165.7 2.7 %fusion.18 = f32[1024,4,128]{2,0,1:T(8,128)} fusion(f32[1024,4,128]{2,0,1:T(8,128)} %scatter-add.26, f32[4,128,256]{1,2,0:T(8,128)} %convolution_bitcast_fusion.10, bf16[128,4,128]{2,1,0:T(4,128)(2,1)S(1)} %copy-done.23, f32[4,128,256]{1,2,0:T(8,128)} %get-tuple-element.139, f32[4,128]{1,0:T(4,128)S(1)} %copy-done.29), kind=kOutput, calls=%fused_computation.44 | convolution fusion | flops 34472704 | bytes 2756608 | tf_op jit(solution)/shard_map/hqk,qhd->khd/dot_general | solution.py:117
  169.9 4.8 %all-to-all-start.4 = ((bf16[8,64,1,512]{3,1,2,0:T(8,128)(2,1)}), bf16[8,64,1,512]{3,1,2,0:T(8,128)(2,1)}, u32[]{:S(2)}, u32[]{:S(2)}) async-start(bf16[8,64,1,512]{3,1,2,0:T(8,128)(2,1)} %bitcast.40), calls=%async_computation.4 | async-start | bytes 1048576 | tf_op jit(solution)/shard_map/all_to_all | solution.py:164
  176.1 2.2 fusion.219
  178.3 1.9 copy.181
  180.2 2.9 %copy.180 = f32[2048,1,256]{2,0,1:T(8,128)} copy(f32[2048,1,256]{0,2,1:T(8,128)} %get-tuple-element.100) | data formatting | bytes 4194304
  184.4 2.1 collective-permute-start.11
  186.4 2.9 %fusion.20 = f32[1024,4,128]{2,0,1:T(8,128)} fusion(f32[1024,4,128]{2,0,1:T(8,128)} %fusion.18, f32[4,128,256]{1,2,0:T(8,128)} %convolution_bitcast_fusion.9, bf16[128,4,128]{2,1,0:T(4,128)(2,1)S(1)} %copy-done.22, f32[4,128,256]{1,2,0:T(8,128)} %get-tuple-element.137, f32[4,128]{1,0:T(4,128)S(1)} %get-tuple-element.136), kind=kOutput, calls=%fused_computation.51 | convolution fusion | flops 34603776 | bytes 3280896 | tf_op jit(solution)/shard_map/hqk,qhd->khd/dot_general | solution.py:117
  189.3 2.9 %fusion.22 = f32[1024,4,128]{2,0,1:T(8,128)} fusion(f32[1024,4,128]{2,0,1:T(8,128)} %fusion.20, f32[4,128,256]{1,2,0:T(8,128)} %convolution_bitcast_fusion.8, bf16[128,4,128]{2,1,0:T(4,128)(2,1)S(1)} %copy-done.20, f32[4,128,256]{1,2,0:T(8,128)} %get-tuple-element.135, f32[4,128]{1,0:T(4,128)S(1)} %get-tuple-element.134), kind=kOutput, calls=%fused_computation.53 | convolution fusion | flops 34603776 | bytes 3280896 | tf_op jit(solution)/shard_map/hqk,qhd->khd/dot_general | solution.py:117
  192.2 3.9 %copy.160 = bf16[1024,4,128]{2,1,0:T(4,128)(2,1)} copy(f32[1024,4,128]{2,0,1:T(8,128)} %fusion.22) | data formatting | bytes 3145728 | tf_op jit(solution)/shard_map/scatter-add | solution.py:116
  197.6 3.0 %fusion.57 = (bf16[512,1,512]{2,1,0:T(2,128)(2,1)S(1)}, f32[512,1,512]{2,1,0:T(1,128)}) fusion(pred[]{:T(512)S(6)} %eq.5, bf16[512,2,512]{2,1,0:T(2,128)(2,1)S(1)} %reshape.503), kind=kLoop, calls=%fused_computation.96 | loop fusion | flops 786432 | bytes 2621441 | tf_op jit(solution)/shard_map/convert_element_type | solution.py:128
  200.9 2.7 %fusion.8 = bf16[2048,256]{1,0:T(8,128)(2,1)} fusion(bf16[2048,256]{1,0:T(8,128)(2,1)} %collective-permute-done.11, f32[2048,1,256]{2,0,1:T(8,128)S(1)} %copy-done, f32[2048,1,256]{2,0,1:T(8,128)S(1)} %copy.181, pred[]{:T(512)S(6)} %eq.5), kind=kLoop, calls=%fused_computation.10 | loop fusion | flops 2097152 | bytes 6291457 | tf_op jit(solution)/shard_map/convert_element_type | solution.py:150
  204.2 1.7 collective-permute-start.5
  205.8 2.4 collective-permute-start.7
  208.6 2.0 fusion.63
  210.6 3.5 %collective-permute-start.9 = (bf16[1,64,1,512]{3,1,2,0:T(8,128)(2,1)S(1)}, bf16[1,64,1,512]{3,1,2,0:T(8,128)(2,1)S(1)}, u32[]{:S(2)}, u32[]{:S(2)}) collective-permute-start(bf16[1,64,1,512]{3,1,2,0:T(8,128)(2,1)S(1)} %get-tuple-element.119), channel_id=1, source_target_pairs={{0,6},{1,7},{2,4},{3,5},{4,2},{5,3},{6,0},{7,1},{8,14},{9,15},{10,... | collective-permute-start | bytes 196616 | tf_op jit(solution)/shard_map/ppermute | solution.py:26
  214.2 4.8 %all-to-all-start.5 = ((bf16[8,64,1,512]{3,1,2,0:T(8,128)(2,1)}), bf16[8,64,1,512]{3,1,2,0:T(8,128)(2,1)S(1)}, u32[]{:S(2)}, u32[]{:S(2)}) async-start(bf16[8,64,1,512]{3,1,2,0:T(8,128)(2,1)} %bitcast.50), calls=%async_computation.5 | async-start | bytes 1048576 | tf_op jit(solution)/shard_map/all_to_all | solution.py:165
  225.2 9.1 %all-to-all-done.5 = bf16[8,64,1,512]{3,1,2,0:T(8,128)(2,1)S(1)} async-done(((bf16[8,64,1,512]{3,1,2,0:T(8,128)(2,1)}), bf16[8,64,1,512]{3,1,2,0:T(8,128)(2,1)S(1)}, u32[]{:S(2)}, u32[]{:S(2)}) %all-to-all-start.5) | async-done | bytes 524320 | tf_op jit(solution)/shard_map/all_to_all | solution.py:165
  236.0 1.8 convert_element_type.141
  (162 shorter events, 52.0 us)
Async XLA Ops:
  7.2 8.9 %copy-start.13 = (bf16[1,128,2048]{2,1,0:T(8,128)(2,1)S(1)}, bf16[1,128,2048]{2,1,0:T(8,128)(2,1)}, u32[]{:S(2)}) copy-start(bf16[1,128,2048]{2,1,0:T(8,128)(2,1)} %param.24) | copy-start | bytes 1572868
  9.6 25.5 %copy-start.14 = (bf16[1,128,2048]{2,1,0:T(8,128)(2,1)S(1)}, bf16[1,128,2048]{2,1,0:T(8,128)(2,1)}, u32[]{:S(2)}) copy-start(bf16[1,128,2048]{2,1,0:T(8,128)(2,1)} %param.22) | copy-start | bytes 1572868
  9.6 21.8 %all-to-all-start.2 = ((bf16[64,8,512]{2,0,1:T(8,128)(2,1)}), bf16[64,8,512]{2,0,1:T(8,128)(2,1)S(1)}, u32[]{:S(2)}, u32[]{:S(2)}) async-start(bf16[64,8,512]{2,0,1:T(8,128)(2,1)} %bitcast.15), calls=%async_computation.2 | async-start | bytes 1048576 | tf_op jit(solution)/shard_map/all_to_all | solution.py:64
  31.4 22.4 %copy-start.15 = (bf16[1,128,2048]{2,1,0:T(8,128)(2,1)S(1)}, bf16[1,128,2048]{2,1,0:T(8,128)(2,1)}, u32[]{:S(2)}) copy-start(bf16[1,128,2048]{2,1,0:T(8,128)(2,1)} %param.21) | copy-start | bytes 1572868
  31.4 18.9 %all-to-all-start.3 = ((bf16[64,8,512]{2,0,1:T(8,128)(2,1)}), bf16[64,8,512]{2,0,1:T(8,128)(2,1)S(1)}, u32[]{:S(2)}, u32[]{:S(2)}) async-start(bf16[64,8,512]{2,0,1:T(8,128)(2,1)} %bitcast.24), calls=%async_computation.3 | async-start | bytes 1048576 | tf_op jit(solution)/shard_map/all_to_all | solution.py:65
  50.4 18.8 %all-to-all-start = ((bf16[64,8,512]{2,0,1:T(8,128)(2,1)}), bf16[64,8,512]{2,0,1:T(8,128)(2,1)S(1)}, u32[]{:S(2)}, u32[]{:S(2)}) async-start(bf16[64,8,512]{2,0,1:T(8,128)(2,1)} %bitcast.1), calls=%async_computation | async-start | bytes 1048576 | tf_op jit(solution)/shard_map/all_to_all | solution.py:63
  69.1 18.8 %all-to-all-start.1 = ((bf16[64,8,512]{2,0,1:T(8,128)(2,1)}), bf16[64,8,512]{2,0,1:T(8,128)(2,1)S(1)}, u32[]{:S(2)}, u32[]{:S(2)}) async-start(bf16[64,8,512]{2,0,1:T(8,128)(2,1)} %bitcast.10), calls=%async_computation.1 | async-start | bytes 1048576 | tf_op jit(solution)/shard_map/all_to_all | solution.py:62
  74.1 30.5 %collective-permute-start = (bf16[512,512]{1,0:T(8,128)(2,1)S(1)}, bf16[512,512]{1,0:T(8,128)(2,1)}, u32[]{:S(2)}, u32[]{:S(2)}) collective-permute-start(bf16[512,512]{1,0:T(8,128)(2,1)S(1)} %bitcast.268), channel_id=1, source_target_pairs={{0,1},{1,0},{2,3},{3,2},{4,5},{5,4},{6,7},{7,6},{8,9},{9,8},{10,11... | collective-permute-start | bytes 1572872 | tf_op jit(solution)/shard_map/ppermute | solution.py:32
  76.1 52.5 %collective-permute-start.1 = (bf16[512,512]{1,0:T(8,128)(2,1)S(1)}, bf16[512,512]{1,0:T(8,128)(2,1)}, u32[]{:S(2)}, u32[]{:S(2)}) collective-permute-start(bf16[512,512]{1,0:T(8,128)(2,1)S(1)} %bitcast.267), channel_id=1, source_target_pairs={{0,1},{1,0},{2,3},{3,2},{4,5},{5,4},{6,7},{7,6},{8,9},{9,8},{10,11... | collective-permute-start | bytes 1572872 | tf_op jit(solution)/shard_map/ppermute | solution.py:32
  89.5 80.4 %all-to-all-start.6 = ((bf16[64,8,2048]{2,0,1:T(8,128)(2,1)}), bf16[64,8,2048]{2,0,1:T(8,128)(2,1)S(1)}, u32[]{:S(2)}, u32[]{:S(2)}) async-start(bf16[64,8,2048]{2,0,1:T(8,128)(2,1)} %bitcast.80), calls=%async_computation.6 | async-start | bytes 4194304 | tf_op jit(solution)/shard_map/all_to_all | solution.py:140
  110.2 6.9 %copy-start.16 = (bf16[256,4,128]{2,1,0:T(4,128)(2,1)}, bf16[256,4,128]{2,1,0:T(4,128)(2,1)S(1)}, u32[]{:S(2)}) copy-start(bf16[256,4,128]{2,1,0:T(4,128)(2,1)S(1)} %slice.303) | copy-start | bytes 786436
  112.3 4.8 %copy-start.19 = (bf16[128,4,128]{2,1,0:T(4,128)(2,1)S(1)}, bf16[128,4,128]{2,1,0:T(4,128)(2,1)}, u32[]{:S(2)}) copy-start(bf16[128,4,128]{2,1,0:T(4,128)(2,1)} %slice.329) | copy-start | bytes 393220
  117.1 4.3 %copy-start.10 = (bf16[128,4,128]{2,1,0:T(4,128)(2,1)S(1)}, bf16[128,4,128]{2,1,0:T(4,128)(2,1)}, u32[]{:S(2)}) copy-start(bf16[128,4,128]{2,1,0:T(4,128)(2,1)} %slice.317) | copy-start | bytes 393220
  121.4 2.7 %copy-start.27 = (f32[4,128]{1,0:T(4,128)}, f32[4,128]{1,0:T(4,128)S(1)}, u32[]{:S(2)}) copy-start(f32[4,128]{1,0:T(4,128)S(1)} %get-tuple-element.138) | copy-start | bytes 6148
  121.4 2.9 %copy-start.21 = (bf16[128,4,128]{2,1,0:T(4,128)(2,1)S(1)}, bf16[128,4,128]{2,1,0:T(4,128)(2,1)}, u32[]{:S(2)}) copy-start(bf16[128,4,128]{2,1,0:T(4,128)(2,1)} %slice.321) | copy-start | bytes 393220
  121.4 4.8 %copy-start.12 = (bf16[128,4,128]{2,1,0:T(4,128)(2,1)S(1)}, bf16[128,4,128]{2,1,0:T(4,128)(2,1)}, u32[]{:S(2)}) copy-start(bf16[128,4,128]{2,1,0:T(4,128)(2,1)} %slice.325) | copy-start | bytes 393220
  124.3 4.3 %copy-start.18 = (bf16[256,4,128]{2,1,0:T(4,128)(2,1)}, bf16[256,4,128]{2,1,0:T(4,128)(2,1)S(1)}, u32[]{:S(2)}) copy-start(bf16[256,4,128]{2,1,0:T(4,128)(2,1)S(1)} %slice.319) | copy-start | bytes 786436
  141.6 3.5 %copy-start.7 = (bf16[256,4,128]{2,1,0:T(4,128)(2,1)S(1)}, bf16[256,4,128]{2,1,0:T(4,128)(2,1)}, u32[]{:S(2)}) copy-start(bf16[256,4,128]{2,1,0:T(4,128)(2,1)} %slice.331) | copy-start | bytes 786436
  144.7 3.9 %copy-start.6 = (bf16[256,4,128]{2,1,0:T(4,128)(2,1)S(1)}, bf16[256,4,128]{2,1,0:T(4,128)(2,1)}, u32[]{:S(2)}) copy-start(bf16[256,4,128]{2,1,0:T(4,128)(2,1)} %slice.323) | copy-start | bytes 786436
  144.8 23.6 %collective-permute-start.3 = (bf16[512,512]{1,0:T(8,128)(2,1)S(1)}, bf16[512,512]{1,0:T(8,128)(2,1)}, u32[]{:S(2)}, u32[]{:S(2)}) collective-permute-start(bf16[512,512]{1,0:T(8,128)(2,1)S(1)} %bitcast.279), channel_id=1, source_target_pairs={{0,1},{1,0},{2,3},{3,2},{4,5},{5,4},{6,7},{7,6},{8,9},{9,8},{10,11... | collective-permute-start | bytes 1572872 | tf_op jit(solution)/shard_map/ppermute | solution.py:32
  148.7 4.7 %copy-start.5 = (bf16[256,4,128]{2,1,0:T(4,128)(2,1)S(1)}, bf16[256,4,128]{2,1,0:T(4,128)(2,1)}, u32[]{:S(2)}) copy-start(bf16[256,4,128]{2,1,0:T(4,128)(2,1)} %slice.315) | copy-start | bytes 786436
  150.7 2.7 %copy-start.11 = (bf16[128,4,128]{2,1,0:T(4,128)(2,1)S(1)}, bf16[128,4,128]{2,1,0:T(4,128)(2,1)}, u32[]{:S(2)}) copy-start(bf16[128,4,128]{2,1,0:T(4,128)(2,1)} %slice.317) | copy-start | bytes 393220
  150.7 3.7 %copy-start.28 = (f32[4,128]{1,0:T(4,128)S(1)}, f32[4,128]{1,0:T(4,128)}, u32[]{:S(2)}) copy-start(f32[4,128]{1,0:T(4,128)} %copy-done.27) | copy-start | bytes 6148
  153.4 3.7 %copy-start.9 = (bf16[128,4,128]{2,1,0:T(4,128)(2,1)S(1)}, bf16[128,4,128]{2,1,0:T(4,128)(2,1)}, u32[]{:S(2)}) copy-start(bf16[128,4,128]{2,1,0:T(4,128)(2,1)} %slice.309) | copy-start | bytes 393220
  157.2 2.6 %copy-start.8 = (f32[4,128,256]{1,2,0:T(8,128)}, f32[4,128,256]{1,2,0:T(8,128)S(1)}, u32[]{:S(2)}) copy-start(f32[4,128,256]{1,2,0:T(8,128)S(1)} %convolution_bitcast_fusion.11) | copy-start | bytes 1572868
  157.3 2.6 %copy-start.25 = (bf16[128,4,128]{2,0,1:T(8,128)(2,1)S(1)}, bf16[128,4,128]{2,0,1:T(8,128)(2,1)}, u32[]{:S(2)}) copy-start(bf16[128,4,128]{2,0,1:T(8,128)(2,1)} %fusion.54) | copy-start | bytes 393220
  157.3 2.6 %copy-start.26 = (bf16[128,4,128]{2,0,1:T(8,128)(2,1)S(1)}, bf16[128,4,128]{2,0,1:T(8,128)(2,1)}, u32[]{:S(2)}) copy-start(bf16[128,4,128]{2,0,1:T(8,128)(2,1)} %fusion.53) | copy-start | bytes 393220
  159.8 2.5 %copy-start.24 = (bf16[128,4,128]{2,1,0:T(4,128)(2,1)S(1)}, bf16[128,4,128]{2,1,0:T(4,128)(2,1)}, u32[]{:S(2)}) copy-start(bf16[128,4,128]{2,1,0:T(4,128)(2,1)} %slice.305) | copy-start | bytes 393220
  162.3 3.4 %copy-start.23 = (bf16[128,4,128]{2,1,0:T(4,128)(2,1)S(1)}, bf16[128,4,128]{2,1,0:T(4,128)(2,1)}, u32[]{:S(2)}) copy-start(bf16[128,4,128]{2,1,0:T(4,128)(2,1)} %slice.313) | copy-start | bytes 393220
  162.3 3.4 %copy-start.29 = (f32[4,128]{1,0:T(4,128)S(1)}, f32[4,128]{1,0:T(4,128)}, u32[]{:S(2)}) copy-start(f32[4,128]{1,0:T(4,128)} %copy-done.27) | copy-start | bytes 6148
  169.9 6.1 %copy-start.1 = (bf16[512,512]{1,0:T(8,128)(2,1)}, bf16[512,512]{1,0:T(8,128)(2,1)S(1)}, u32[]{:S(2)}) copy-start(bf16[512,512]{1,0:T(8,128)(2,1)S(1)} %fusion.62) | copy-start | bytes 1572868
  169.9 44.2 %all-to-all-start.4 = ((bf16[8,64,1,512]{3,1,2,0:T(8,128)(2,1)}), bf16[8,64,1,512]{3,1,2,0:T(8,128)(2,1)}, u32[]{:S(2)}, u32[]{:S(2)}) async-start(bf16[8,64,1,512]{3,1,2,0:T(8,128)(2,1)} %bitcast.40), calls=%async_computation.4 | async-start | bytes 1048576 | tf_op jit(solution)/shard_map/all_to_all | solution.py:164
  174.7 61.2 %reduce-scatter.2.cloned.1.call-start = ((), (), s32[]{:S(2)}) async-start(), calls=%async_computation.8 | async-start | bytes 1310720 | tf_op jit(solution)/shard_map/reduce_scatter | solution.py:149
  183.1 3.3 %copy-start.22 = (bf16[128,4,128]{2,1,0:T(4,128)(2,1)S(1)}, bf16[128,4,128]{2,1,0:T(4,128)(2,1)}, u32[]{:S(2)}) copy-start(bf16[128,4,128]{2,1,0:T(4,128)(2,1)} %slice.321) | copy-start | bytes 393220
  184.4 4.9 %copy-start.20 = (bf16[128,4,128]{2,1,0:T(4,128)(2,1)S(1)}, bf16[128,4,128]{2,1,0:T(4,128)(2,1)}, u32[]{:S(2)}) copy-start(bf16[128,4,128]{2,1,0:T(4,128)(2,1)} %slice.329) | copy-start | bytes 393220
  184.4 16.5 %collective-permute-start.11 = (bf16[2048,256]{1,0:T(8,128)(2,1)}, bf16[2048,256]{1,0:T(8,128)(2,1)}, u32[]{:S(2)}, u32[]{:S(2)}) collective-permute-start(bf16[2048,256]{1,0:T(8,128)(2,1)} %fusion.61), channel_id=1, source_target_pairs={{0,1},{1,0},{2,3},{3,2},{4,5},{5,4},{6,7},{7,6},{8,9},{9,8},{10,11... | collective-permute-start | bytes 3145736 | tf_op jit(solution)/shard_map/ppermute | solution.py:32
  197.6 3.3 %copy-start = (f32[2048,1,256]{2,0,1:T(8,128)S(1)}, f32[2048,1,256]{2,0,1:T(8,128)}, u32[]{:S(2)}) copy-start(f32[2048,1,256]{2,0,1:T(8,128)} %copy.180) | copy-start | bytes 6291460
  200.8 2.8 %copy-start.2 = (bf16[512,512]{1,0:T(8,128)(2,1)S(1)}, bf16[512,512]{1,0:T(8,128)(2,1)}, u32[]{:S(2)}) copy-start(bf16[512,512]{1,0:T(8,128)(2,1)} %copy-done.1) | copy-start | bytes 1572868
  200.8 7.5 %collective-permute-start.2 = (bf16[512,512]{1,0:T(8,128)(2,1)S(1)}, bf16[512,512]{1,0:T(8,128)(2,1)}, u32[]{:S(2)}, u32[]{:S(2)}) collective-permute-start(bf16[512,512]{1,0:T(8,128)(2,1)S(1)} %bitcast.278), channel_id=1, source_target_pairs={{0,1},{1,0},{2,3},{3,2},{4,5},{5,4},{6,7},{7,6},{8,9},{9,8},{10,11... | collective-permute-start | bytes 1572872 | tf_op jit(solution)/shard_map/ppermute | solution.py:32
  203.6 5.0 %copy-start.3 = (f32[512,1,512]{2,1,0:T(1,128)S(1)}, f32[512,1,512]{2,1,0:T(1,128)}, u32[]{:S(2)}) copy-start(f32[512,1,512]{2,1,0:T(1,128)} %get-tuple-element.105) | copy-start | bytes 3145732
  203.7 6.9 %collective-permute-start.4 = (bf16[1,64,1,512]{3,1,2,0:T(8,128)(2,1)S(1)}, bf16[1,64,1,512]{3,1,2,0:T(8,128)(2,1)S(1)}, u32[]{:S(2)}, u32[]{:S(2)}) collective-permute-start(bf16[1,64,1,512]{3,1,2,0:T(8,128)(2,1)S(1)} %get-tuple-element.124), channel_id=1, source_target_pairs={{0,1},{1,0},{2,3},{3,2},{4,5},{5,4},{6,7},{7,6},{8,9},{9,8},{10,11... | collective-permute-start | bytes 196616 | tf_op jit(solution)/shard_map/ppermute | solution.py:26
  204.2 9.9 %collective-permute-start.5 = (bf16[1,64,1,512]{3,1,2,0:T(8,128)(2,1)S(1)}, bf16[1,64,1,512]{3,1,2,0:T(8,128)(2,1)S(1)}, u32[]{:S(2)}, u32[]{:S(2)}) collective-permute-start(bf16[1,64,1,512]{3,1,2,0:T(8,128)(2,1)S(1)} %get-tuple-element.123), channel_id=1, source_target_pairs={{0,2},{1,3},{2,0},{3,1},{4,6},{5,7},{6,4},{7,5},{8,10},{9,11},{10,... | collective-permute-start | bytes 196616 | tf_op jit(solution)/shard_map/ppermute | solution.py:26
  205.8 13.2 %collective-permute-start.6 = (bf16[1,64,1,512]{3,1,2,0:T(8,128)(2,1)S(1)}, bf16[1,64,1,512]{3,1,2,0:T(8,128)(2,1)S(1)}, u32[]{:S(2)}, u32[]{:S(2)}) collective-permute-start(bf16[1,64,1,512]{3,1,2,0:T(8,128)(2,1)S(1)} %get-tuple-element.122), channel_id=1, source_target_pairs={{0,3},{1,2},{2,1},{3,0},{4,7},{5,6},{6,5},{7,4},{8,11},{9,10},{10,... | collective-permute-start | bytes 196616 | tf_op jit(solution)/shard_map/ppermute | solution.py:26
  205.8 13.2 %collective-permute-start.7 = (bf16[1,64,1,512]{3,1,2,0:T(8,128)(2,1)S(1)}, bf16[1,64,1,512]{3,1,2,0:T(8,128)(2,1)S(1)}, u32[]{:S(2)}, u32[]{:S(2)}) collective-permute-start(bf16[1,64,1,512]{3,1,2,0:T(8,128)(2,1)S(1)} %get-tuple-element.121), channel_id=1, source_target_pairs={{0,4},{1,5},{2,6},{3,7},{4,0},{5,1},{6,2},{7,3},{8,12},{9,13},{10,... | collective-permute-start | bytes 196616 | tf_op jit(solution)/shard_map/ppermute | solution.py:26
  208.2 10.8 %collective-permute-start.8 = (bf16[1,64,1,512]{3,1,2,0:T(8,128)(2,1)S(1)}, bf16[1,64,1,512]{3,1,2,0:T(8,128)(2,1)S(1)}, u32[]{:S(2)}, u32[]{:S(2)}) collective-permute-start(bf16[1,64,1,512]{3,1,2,0:T(8,128)(2,1)S(1)} %get-tuple-element.120), channel_id=1, source_target_pairs={{0,5},{1,4},{2,7},{3,6},{4,1},{5,0},{6,3},{7,2},{8,13},{9,12},{10,... | collective-permute-start | bytes 196616 | tf_op jit(solution)/shard_map/ppermute | solution.py:26
  210.6 8.5 %collective-permute-start.9 = (bf16[1,64,1,512]{3,1,2,0:T(8,128)(2,1)S(1)}, bf16[1,64,1,512]{3,1,2,0:T(8,128)(2,1)S(1)}, u32[]{:S(2)}, u32[]{:S(2)}) collective-permute-start(bf16[1,64,1,512]{3,1,2,0:T(8,128)(2,1)S(1)} %get-tuple-element.119), channel_id=1, source_target_pairs={{0,6},{1,7},{2,4},{3,5},{4,2},{5,3},{6,0},{7,1},{8,14},{9,15},{10,... | collective-permute-start | bytes 196616 | tf_op jit(solution)/shard_map/ppermute | solution.py:26
  214.1 6.3 %collective-permute-start.10 = (bf16[1,64,1,512]{3,1,2,0:T(8,128)(2,1)S(1)}, bf16[1,64,1,512]{3,1,2,0:T(8,128)(2,1)S(1)}, u32[]{:S(2)}, u32[]{:S(2)}) collective-permute-start(bf16[1,64,1,512]{3,1,2,0:T(8,128)(2,1)S(1)} %get-tuple-element.118), channel_id=1, source_target_pairs={{0,7},{1,6},{2,5},{3,4},{4,3},{5,2},{6,1},{7,0},{8,15},{9,14},{10,... | collective-permute-start | bytes 196616 | tf_op jit(solution)/shard_map/ppermute | solution.py:26
  214.2 20.2 %all-to-all-start.5 = ((bf16[8,64,1,512]{3,1,2,0:T(8,128)(2,1)}), bf16[8,64,1,512]{3,1,2,0:T(8,128)(2,1)S(1)}, u32[]{:S(2)}, u32[]{:S(2)}) async-start(bf16[8,64,1,512]{3,1,2,0:T(8,128)(2,1)} %bitcast.50), calls=%async_computation.5 | async-start | bytes 1048576 | tf_op jit(solution)/shard_map/all_to_all | solution.py:165
  (2 other events, 3.1 us)
Sparse Core Ops, SparseCore 0:
  203.7 28.9 reduce-scatter.1
